TPU v7x, 128 devices: a whole 4x4x4 slice. The times are simulated.
128 devices in a mesh: row: 16 (over x, y_lo, core), col: 8 (over y_hi, z).
Axes of the slice: x: 4, y: 4 (y_hi: 2, y_lo: 2; y = y_hi * 2 + y_lo), z: 4, core: 2. Of those that a mesh axis runs over, the one named last changes fastest.
Arguments:
- pair_in: bfloat16 [768, 768, 128], P('row', 'col'), may hold values from -6 to 6
- coords: float32 [3, 768], P(None, 'row'), may hold values from -36 to 36
- chain_ids: int32 [768], P('row'), may hold values from 0 to 3, never falling along the last dimension, each value on 1 to 384 neighbouring positions
- coord_mask: int32 [768], P('row'), may hold values 0 or 1
- gain_tri: float32 [128], replicated, may hold values from 0.1 to 1.9
- gain_sum: float32 [128], replicated, may hold values from 0.1 to 1.9
- gain_attn: float32 [128], replicated, may hold values from 0.1 to 1.9
- w_tri_in: bfloat16 [128, 640], replicated, may hold values from -0.5 to 0.5
- w_tri_out: bfloat16 [128, 128], replicated, may hold values from -0.5 to 0.5
- w_bins: float32 [36, 128], replicated, may hold values from -3 to 3
- same_chain: float32 [128], replicated, may hold values from -6 to 6
- w_query: bfloat16 [128, 128], replicated, may hold values from -8 to 8
- w_attn: bfloat16 [128, 384], replicated, may hold values from -0.5 to 0.5
- w_bias: bfloat16 [128, 4], replicated, may hold values from -0.5 to 0.5
- w_attn_out: bfloat16 [128, 128], replicated, may hold values from -0.5 to 0.5
Outputs:
- pair_out: bfloat16 [768, 768, 128], P('row', 'col')
Inputs may be any that keep to these rules, and one draw needn't show every extreme that they name: `chain_ids`: chain numbers never fall along the residues, and no chain holds more than half of them.
All inputs are finite; a program needn't handle non-finite values. No bound on the sum of `coord_mask` on one device may be relied on, other than what follows from the above.
Results may differ from a plain program's by a relative error of at most 0.02.
Values may be sent and summed in bfloat16 or wider, within the bound.
No kernel may reach another device: no remote copies, remote signals or barrier semaphores. Data moves between devices by JAX's collectives and lax.ppermute only.
A program may use at most 192 MiB of HBM per device.

v0:
```python
import math

import jax
import jax.numpy as jnp
from jax import lax
from jax.sharding import PartitionSpec as P


def joined_along(tiles, dim):
    lengths = list(tiles.shape[1:])
    lengths[dim] *= tiles.shape[0]
    return jnp.moveaxis(tiles, 0, dim).reshape(lengths)


def from_everyone(array, axis):
    copies = jnp.broadcast_to(array, (lax.axis_size(axis), *array.shape))
    return lax.all_to_all(copies, axis, split_axis=0, concat_axis=0, tiled=True)


def gather_directly(array, axis, dim):
    return joined_along(from_everyone(array, axis), dim)


def layer_norm(values, gain):
    center = values - jnp.mean(values, axis=-1, keepdims=True)
    spread = jnp.mean(center * center, axis=-1, keepdims=True)
    return center * lax.rsqrt(spread + 1e-05) * gain


def body(
    pair_in,
    coords,
    chain_ids,
    coord_mask,
    gain_tri,
    gain_sum,
    gain_attn,
    w_tri_in,
    w_tri_out,
    w_bins,
    same_chain,
    w_query,
    w_attn,
    w_bias,
    w_attn_out,
):
    n_rows = lax.axis_size("row")
    n_cols = lax.axis_size("col")
    row_count, col_count, channels = pair_in.shape
    n_heads = w_bias.shape[1]
    head_size = channels // n_heads
    n_bins = w_bins.shape[0]
    total_res = row_count * n_rows
    stride = col_count // n_rows
    col_start = lax.axis_index("col") * col_count
    coords_all, chains_all, masks_all = (
        gather_directly(coords, "row", 1),
        gather_directly(chain_ids, "row", 0),
        gather_directly(coord_mask, "row", 0),
    )
    pair_wide = pair_in.astype(jnp.float32)
    normed = layer_norm(pair_wide, gain_tri).astype(jnp.bfloat16)
    projected = jnp.dot(
        normed.reshape(row_count * col_count, channels),
        w_tri_in,
        preferred_element_type=jnp.float32,
    ).reshape(row_count, col_count, 5 * channels)
    left_side = (
        (jax.nn.sigmoid(projected[..., :channels]) * projected[..., channels : 2 * channels])
        .astype(jnp.bfloat16)
        .transpose(2, 0, 1)
    )
    right_side = (
        (
            jax.nn.sigmoid(projected[..., 2 * channels : 3 * channels])
            * projected[..., 3 * channels : 4 * channels]
        )
        .astype(jnp.bfloat16)
        .transpose(2, 0, 1)
    )
    tri_gate = jax.nn.sigmoid(projected[..., 4 * channels :])
    left_rows = lax.all_gather(left_side, "col", axis=2, tiled=True)
    left_perm = (
        left_rows.reshape(channels, row_count, n_cols, n_rows, stride)
        .transpose(0, 1, 3, 2, 4)
        .reshape(channels, row_count, total_res)
    )
    moved = lax.all_to_all(
        lax.all_to_all(right_side, "row", split_axis=2, concat_axis=1, tiled=True),
        "col",
        split_axis=1,
        concat_axis=2,
        tiled=True,
    )
    product = jnp.einsum(
        "cik,cjk->cij",
        left_perm,
        lax.all_gather(moved, "row", axis=2, tiled=True),
        preferred_element_type=jnp.float32,
    ).transpose(1, 2, 0)
    summed_norm = layer_norm(product, gain_sum).astype(jnp.bfloat16)
    pair_one = pair_wide + tri_gate * jnp.dot(
        summed_norm.reshape(row_count * col_count, channels),
        w_tri_out,
        preferred_element_type=jnp.float32,
    ).reshape(row_count, col_count, channels)
    far_coords = lax.dynamic_slice_in_dim(coords_all, col_start, col_count, 1)
    far_chains = lax.dynamic_slice_in_dim(chains_all, col_start, col_count, 0)
    far_masks = lax.dynamic_slice_in_dim(masks_all, col_start, col_count, 0)
    offsets = coords[:, :, None] - far_coords[:, None, :]
    dist = jnp.sqrt(jnp.sum(offsets * offsets, axis=0) + 1.0)
    centres = 2.0 + 20.0 * jnp.arange(n_bins, dtype=jnp.float32) / (n_bins - 1)
    spacing = 25.0 / (n_bins - 1)
    pair_mask = coord_mask.astype(jnp.float32)[:, None] * far_masks.astype(jnp.float32)[None, :]
    feats = jnp.exp(-(((dist[..., None] - centres) / spacing) ** 2)) * pair_mask[..., None]
    binned = jnp.dot(feats.reshape(row_count * col_count, n_bins), w_bins).reshape(
        row_count, col_count, channels
    )
    shared = (chain_ids[:, None] == far_chains[None, :]).astype(jnp.float32)
    pair_two = (pair_one + binned + shared[..., None] * same_chain).astype(jnp.bfloat16)
    normed_two = layer_norm(pair_two.astype(jnp.float32), gain_attn).astype(jnp.bfloat16)
    flat_two = normed_two.reshape(row_count * col_count, channels)
    queries = (
        jnp.dot(flat_two, w_query, preferred_element_type=jnp.float32)
        .astype(jnp.bfloat16)
        .reshape(row_count, col_count, n_heads, head_size)
    )
    gate_pre = jnp.dot(
        flat_two, w_attn[:, 2 * channels :], preferred_element_type=jnp.float32
    ).reshape(row_count, col_count, channels)
    attn_gate = jax.nn.sigmoid(gate_pre)
    pair_bias = (
        jnp.dot(flat_two, w_bias, preferred_element_type=jnp.float32)
        .astype(jnp.bfloat16)
        .reshape(row_count, col_count, n_heads)
        .transpose(2, 0, 1)
    )
    bias_moved = lax.all_to_all(
        lax.all_to_all(pair_bias, "row", split_axis=2, concat_axis=1, tiled=True),
        "col",
        split_axis=1,
        concat_axis=2,
        tiled=True,
    )
    bias_gathered = gather_directly(bias_moved, "row", 2)
    bias_mine = (
        bias_gathered.reshape(n_heads, col_count, n_rows, n_cols, stride)
        .transpose(0, 1, 3, 2, 4)
        .reshape(n_heads, col_count, total_res)
    )
    group = math.gcd(row_count, 8)
    blocks = row_count // group
    query_groups = queries.reshape(blocks, group, col_count, n_heads, head_size)
    root_dim = math.sqrt(head_size)
    start_state = (
        jnp.full((blocks, group, n_heads, col_count), -1e30, jnp.float32),
        jnp.zeros((blocks, group, n_heads, col_count), jnp.float32),
        jnp.zeros((blocks, group, n_heads, col_count, head_size), jnp.float32),
    )
    panel = lax.all_gather(normed_two, "col", axis=1, tiled=True)
    span = panel.shape[1]
    both = jnp.dot(
        panel.reshape(row_count * span, channels),
        w_attn[:, : 2 * channels],
        preferred_element_type=jnp.float32,
    ).reshape(row_count, span, 2 * channels)
    key_part = both[..., :channels].astype(jnp.bfloat16)
    span = key_part.shape[1]
    bias_part = bias_mine.astype(jnp.float32)
    key_groups = key_part.reshape(blocks, group, span, n_heads, head_size)
    value_groups = (
        both[..., channels:].astype(jnp.bfloat16).reshape(blocks, group, span, n_heads, head_size)
    )

    def one_block(items):
        query_blk, key_blk, value_blk, running_top, running_total, running_acc = items
        scores = (
            jnp.einsum("ijhd,ikhd->ihjk", query_blk, key_blk, preferred_element_type=jnp.float32)
            / root_dim
            + bias_part[None]
        )
        new_top = jnp.maximum(running_top, jnp.max(scores, axis=-1))
        rescale = jnp.exp(running_top - new_top)
        expo = jnp.exp(scores - new_top[..., None])
        new_total = running_total * rescale + jnp.sum(expo, axis=-1)
        new_acc = running_acc * rescale[..., None] + jnp.einsum(
            "ihjk,ikhd->ihjd",
            expo.astype(jnp.bfloat16),
            value_blk,
            preferred_element_type=jnp.float32,
        )
        return (new_top, new_total, new_acc)

    final_top, final_total, final_acc = lax.map(
        one_block,
        (query_groups, key_groups, value_groups, start_state[0], start_state[1], start_state[2]),
    )
    attended = (
        (final_acc / final_total[..., None])
        .reshape(row_count, n_heads, col_count, head_size)
        .transpose(0, 2, 1, 3)
        .reshape(row_count, col_count, channels)
    )
    gated = (attn_gate * attended).astype(jnp.bfloat16)
    result = pair_two.astype(jnp.float32) + jnp.dot(
        gated.reshape(row_count * col_count, channels),
        w_attn_out,
        preferred_element_type=jnp.float32,
    ).reshape(row_count, col_count, channels)
    return result.astype(jnp.bfloat16)


def solution(mesh):
    return jax.shard_map(
        body,
        mesh=mesh,
        in_specs=(
            P("row", "col", None),
            P(None, "row"),
            P("row"),
            P("row"),
            P(),
            P(),
            P(),
            P(),
            P(),
            P(),
            P(),
            P(),
            P(),
            P(),
            P(),
        ),
        out_specs=P("row", "col", None),
        check_vma=False,
    )
```

profile of v0, /device:TPU:1, one launch (start us, length us, event | category | flops | bytes accessed | tf_op | source)
XLA Modules:
  0.0 541.1 jit_solution(7241919329803855443)
XLA Ops:
  6.5 1.9 convert_reduce_fusion.1
  8.4 2.7 fusion.35
  11.2 2.0 fusion.56
  13.2 2.8 fusion.63
  16.1 1.8 copy-done.2
  18.4 24.0 %all_to_all.94 = bf16[128,48,96]{0,1,2:T(8,128)(2,1)S(1)} all-to-all(bf16[128,48,96]{0,1,2:T(8,128)(2,1)S(1)} %copy.109), channel_id=1, replica_groups=mesh['row'=16,'col'=8] {'row'}, dimensions={2} | all-to-all | bytes 2359296 | tf_op jit(solution)/shard_map/all_to_all | solution.py:89
  42.5 0.8 copy.111
  43.4 32.2 %all_to_all.95 = bf16[128,768,6]{0,2,1:T(8,128)(2,1)S(1)} all-to-all(bf16[128,768,6]{0,2,1:T(8,128)(2,1)S(1)} %copy.111), channel_id=1, replica_groups=mesh['row'=16,'col'=8] {'col'}, dimensions={1} | all-to-all | bytes 2359296 | tf_op jit(solution)/shard_map/all_to_all | solution.py:88
  75.8 1.8 copy.114
  77.6 12.5 %all_to_all.96 = s32[16,1,48]{2,1,0:T(1,128)S(1)} all-to-all(s32[16,1,48]{2,1,0:T(1,128)S(1)} %broadcast_in_dim.13), channel_id=1, replica_groups=mesh['row'=16,'col'=8] {'row'}, dimensions={0} | all-to-all | bytes 6144 | tf_op jit(solution)/shard_map/all_to_all | solution.py:17
  90.7 3.8 all-to-all-start.4
  96.6 3.6 all-to-all-done.4
  100.2 3.9 all-to-all-start.2
  105.3 4.7 all-to-all-done.2
  111.7 47.2 %all-gather.4.cloned.1.call-done = bf16[128,48,768]{0,2,1:T(8,128)(2,1)} async-done(((bf16[128,48,96]{0,2,1:T(8,128)(2,1)}), bf16[128,48,768]{0,2,1:T(8,128)(2,1)}) %all-gather.4.cloned.1.call-update) | async-done | bytes 9437200 | tf_op jit(solution)/shard_map/all_gather | solution.py:82
  158.9 13.4 %copy.107 = bf16[128,48,768]{0,1,2:T(8,128)(2,1)} copy(bf16[128,48,768]{0,2,1:T(8,128)(2,1)} %all-gather.4.cloned.1.call-done) | data formatting | bytes 18874368 | tf_op jit(solution)/shard_map/all_gather | solution.py:82
  172.2 10.0 %copy.108 = bf16[128,48,16,8,6]{0,1,4,3,2:T(8,128)(2,1)} copy(bf16[128,48,16,8,6]{0,1,4,2,3:T(8,128)(2,1)} %bitcast.128) | data formatting | bytes 18874368 | tf_op jit(solution)/shard_map/transpose | solution.py:85
  182.2 14.4 %copy.115 = bf16[128,48,768]{2,1,0:T(8,128)(2,1)} copy(bf16[128,48,768]{0,1,2:T(8,128)(2,1)} %bitcast.129) | data formatting | bytes 18874368 | tf_op jit(solution)/shard_map/reshape | solution.py:86
  196.6 93.9 %all-gather.6.cloned.1.call-done = bf16[128,96,768]{1,2,0:T(8,128)(2,1)} async-done(((bf16[128,96,48]{1,2,0:T(8,128)(2,1)}), bf16[128,96,768]{1,2,0:T(8,128)(2,1)}) %all-gather.6.cloned.1.call-update) | async-done | bytes 18874384 | tf_op jit(solution)/shard_map/all_gather | solution.py:98
  290.5 13.3 %bitcast_reduce_fusion = (f32[48,96]{1,0:T(8,128)S(1)}, f32[128,48,96]{2,1,0:T(8,128)S(1)}) fusion(bf16[128,48,768]{2,1,0:T(8,128)(2,1)} %copy.115, bf16[128,96,768]{1,2,0:T(8,128)(2,1)} %all-gather.6.cloned.1.call-done), kind=kOutput, calls=%fused_computation.32 | convolution fusion | flops 906554880 | bytes 30689280 | tf_op jit(solution)/shard_map/cik,cjk->cij/dot_general | solution.py:95
  306.5 3.8 convert_reduce_fusion
  310.3 1.6 fusion.32
  312.0 2.5 fusion.34
  314.5 1.7 convolution_convert_fusion.2
  316.6 10.8 %all_to_all.97 = bf16[16,2,576]{2,1,0:T(2,128)(2,1)S(1)} all-to-all(bf16[16,2,576]{2,1,0:T(2,128)(2,1)S(1)} %reshape.272), channel_id=1, replica_groups=mesh['row'=16,'col'=8] {'row'}, dimensions={0} | all-to-all | bytes 73728 | tf_op jit(solution)/shard_map/all_to_all | solution.py:139
  328.3 1.2 reshape.274
  329.5 13.1 %all_to_all.98 = bf16[8,2,1152]{2,1,0:T(2,128)(2,1)S(1)} all-to-all(bf16[8,2,1152]{2,1,0:T(2,128)(2,1)S(1)} %reshape.274), channel_id=1, replica_groups=mesh['row'=16,'col'=8] {'col'}, dimensions={0} | all-to-all | bytes 73728 | tf_op jit(solution)/shard_map/all_to_all | solution.py:138
  342.6 1.7 reshape.275
  344.9 1.0 broadcast_in_dim.15
  345.9 5.6 %all-to-all-start.7 = ((bf16[16,4,96,48]{2,3,1,0:T(8,128)(2,1)}), bf16[16,4,96,48]{2,3,1,0:T(8,128)(2,1)S(1)}, u32[]{:S(2)}, u32[]{:S(2)}) async-start(bf16[16,4,96,48]{2,3,1,0:T(8,128)(2,1)} %broadcast_in_dim.15), calls=%async_computation.7 | async-start | bytes 1572864 | tf_op jit(solution)/shard_map/all_to_all | solution.py:17
  352.6 2.5 reshape_reshape.4
  355.0 8.5 %all-to-all-done.7 = bf16[16,4,96,48]{2,3,1,0:T(8,128)(2,1)S(1)} async-done(((bf16[16,4,96,48]{2,3,1,0:T(8,128)(2,1)}), bf16[16,4,96,48]{2,3,1,0:T(8,128)(2,1)S(1)}, u32[]{:S(2)}, u32[]{:S(2)}) %all-to-all-start.7) | async-done | bytes 589856 | tf_op jit(solution)/shard_map/all_to_all | solution.py:17
  364.0 1.0 copy.126
  365.7 65.1 %all-gather.8.cloned.1.call-done = bf16[48,768,128]{2,1,0:T(8,128)(2,1)} async-done(((bf16[48,96,128]{2,1,0:T(8,128)(2,1)}), bf16[48,768,128]{2,1,0:T(8,128)(2,1)}) %all-gather.8.cloned.1.call-update) | async-done | bytes 9437200 | tf_op jit(solution)/shard_map/all_gather | solution.py:160
  430.8 11.4 %convolution_convert_fusion = bf16[48,768,256]{1,2,0:T(8,128)(2,1)} fusion(bf16[48,768,128]{2,1,0:T(8,128)(2,1)} %all-gather.8.cloned.1.call-done, bf16[128,384]{1,0:T(8,128)(2,1)S(1)} %copy-done.7), kind=kOutput, calls=%fused_computation.22 | convolution fusion | flops 2425356288 | bytes 28377088 | tf_op jit(solution)/shard_map/dot_general | solution.py:162
  442.2 14.3 %fusion.89 = (bf16[48,768,128]{1,2,0:T(8,128)(2,1)}, bf16[48,768,128]{1,2,0:T(8,128)(2,1)}) fusion(bf16[48,768,256]{1,2,0:T(8,128)(2,1)} %convolution_convert_fusion), kind=kLoop, calls=%fused_computation.111 | loop fusion | bytes 37748736 | tf_op jit(solution)/shard_map/slice | solution.py:172
  456.5 68.5 %while.12 = (s32[]{:T(128)}, f32[6,8,4,96]{3,2,1,0:T(4,128)S(1)}, f32[6,8,4,96,32]{3,4,2,1,0:T(8,128)}, bf16[6,8,96,4,32]{2,1,0,4,3:T(8,128)(2,1)}, bf16[6,8,768...) while((s32[]{:T(128)}, f32[6,8,4,96]{3,2,1,0:T(4,128)S(1)}, ...), condition=%wide.region_10.11_spmd, body=%wide.region_7.10_spmd.sunk | while | flops 328055808 | bytes 36259420 | solution.py:194
  456.5 1.0 constant_dynamic-slice_fusion.3
  457.5 3.0 fusion.108
  460.5 5.0 fusion.110
  465.5 2.4 fusion.109
  468.0 1.0 constant_dynamic-slice_fusion.3
  468.9 3.0 fusion.108
  472.0 5.0 fusion.110
  477.0 2.4 fusion.109
  479.4 1.0 constant_dynamic-slice_fusion.3
  480.4 3.0 fusion.108
  483.4 5.0 fusion.110
  488.4 2.4 fusion.109
  490.8 1.0 constant_dynamic-slice_fusion.3
  491.8 3.0 fusion.108
  494.8 4.9 fusion.110
  499.8 2.4 fusion.109
  502.2 1.0 constant_dynamic-slice_fusion.3
  503.2 3.0 fusion.108
  506.2 5.0 fusion.110
  511.2 2.4 fusion.109
  513.7 1.0 constant_dynamic-slice_fusion.3
  514.7 3.0 fusion.108
  517.7 4.9 fusion.110
  522.6 2.4 fusion.109
  525.1 2.4 broadcast_divide_fusion
  527.5 2.2 copy.129
  529.7 4.4 fusion.41
  (105 shorter events, 13.4 us)
Async XLA Ops:
  6.5 4.6 copy-start
  6.5 4.6 copy-start.4
  6.5 4.6 copy-start.13
  6.5 152.3 %all-gather.4.cloned.1.call-start = ((), (), s32[]{:S(2)}) async-start(), calls=%async_computation.8 | async-start | bytes 10616832 | tf_op jit(solution)/shard_map/all_gather | solution.py:82
  13.2 4.7 copy-start.2
  17.9 272.6 %all-gather.6.cloned.1.call-start = ((), (), s32[]{:S(2)}) async-start(), calls=%async_computation.9 | async-start | bytes 26738688 | tf_op jit(solution)/shard_map/all_gather | solution.py:98
  75.7 1.8 copy-start.15
  75.7 14.4 %copy-start.11 = (s32[48]{0:T(128)S(1)}, s32[48]{0:T(128)}, u32[]{:S(2)}) copy-start(s32[48]{0:T(128)} %param.19) | copy-start | bytes 580
  75.8 18.8 %copy-start.10 = (f32[3,48]{1,0:T(4,128)S(1)}, f32[3,48]{1,0:T(4,128)}, u32[]{:S(2)}) copy-start(f32[3,48]{1,0:T(4,128)} %param.18) | copy-start | bytes 1732
  90.7 9.5 %all-to-all-start.4 = ((s32[16,1,48]{2,1,0:T(1,128)}), s32[16,1,48]{2,1,0:T(1,128)S(1)}, u32[]{:S(2)}, u32[]{:S(2)}) async-start(s32[16,1,48]{2,1,0:T(1,128)} %broadcast_in_dim.14), calls=%async_computation.4 | async-start | bytes 16384 | tf_op jit(solution)/shard_map/all_to_all | solution.py:17
  100.2 9.8 %all-to-all-start.2 = ((f32[16,1,144]{2,1,0:T(1,128)}), f32[16,1,144]{2,1,0:T(1,128)S(1)}, u32[]{:S(2)}, u32[]{:S(2)}) async-start(f32[16,1,144]{2,1,0:T(1,128)} %reshape.270), calls=%async_computation.2 | async-start | bytes 32768 | tf_op jit(solution)/shard_map/all_to_all | solution.py:17
  104.1 326.7 %all-gather.8.cloned.1.call-start = ((), (), s32[]{:S(2)}) async-start(), calls=%async_computation.10 | async-start | bytes 10616832 | tf_op jit(solution)/shard_map/all_gather | solution.py:160
  303.8 0.7 copy-start.14
  304.5 0.8 copy-start.8
  305.2 1.3 copy-start.5
  305.2 1.3 copy-start.18
  305.2 1.3 copy-start.19
  306.5 5.5 %copy-start.16 = (f32[128]{0:T(128)S(1)}, f32[128]{0:T(128)}, u32[]{:S(2)}) copy-start(f32[128]{0:T(128)} %param.23) | copy-start | bytes 1540
  310.3 1.7 copy-start.6
  310.3 4.2 copy-start.12
  328.3 23.2 %copy-start.3 = (bf16[48,96,128]{2,1,0:T(8,128)(2,1)S(1)}, bf16[48,96,128]{2,1,0:T(8,128)(2,1)}, u32[]{:S(2)}) copy-start(bf16[48,96,128]{2,1,0:T(8,128)(2,1)} %fusion.34) | copy-start | bytes 3538948
  328.3 23.2 %copy-start.9 = (bf16[128,128]{1,0:T(8,128)(2,1)S(1)}, bf16[128,128]{1,0:T(8,128)(2,1)}, u32[]{:S(2)}) copy-start(bf16[128,128]{1,0:T(8,128)(2,1)} %param.28) | copy-start | bytes 98308
  345.9 17.7 %all-to-all-start.7 = ((bf16[16,4,96,48]{2,3,1,0:T(8,128)(2,1)}), bf16[16,4,96,48]{2,3,1,0:T(8,128)(2,1)S(1)}, u32[]{:S(2)}, u32[]{:S(2)}) async-start(bf16[16,4,96,48]{2,3,1,0:T(8,128)(2,1)} %broadcast_in_dim.15), calls=%async_computation.7 | async-start | bytes 1572864 | tf_op jit(solution)/shard_map/all_to_all | solution.py:17
  364.0 66.8 %copy-start.7 = (bf16[128,384]{1,0:T(8,128)(2,1)S(1)}, bf16[128,384]{1,0:T(8,128)(2,1)}, u32[]{:S(2)}) copy-start(bf16[128,384]{1,0:T(8,128)(2,1)} %param.29) | copy-start | bytes 294916
  527.5 2.2 copy-start.17
  529.7 4.4 copy-start.1
Sparse Core Ops, SparseCore 0:
  18.0 140.8 all-gather.3
  160.5 129.8 all-gather.5
  314.6 116.1 all-gather.7
where the time goes:
time: 549 us; the launch traced here: 541 us
  waiting for transfers between devices  223 us (41%)
  blocking collectives  92.6 us (17%)
  matrix products  85.4 us (16%)
  local copies, waits for them, and re-layouts  79.8 us (15%)
  other arithmetic  32.5 us (6%)
  between operations  14.1 us (3%)
  starting transfers between devices  13.6 us (2%)
    all_gather x1, waiting for transfers between devices, body(): lax.all_gather(moved, 'row', axis=2, tiled=True)  93.9 us
    all_gather x1, waiting for transfers between devices, body(): panel = lax.all_gather(normed_two, 'col', axis=1, tiled=True)  65.1 us
    all_gather x1, waiting for transfers between devices, body(): left_rows = lax.all_gather(left_side, 'col', axis=2, tiled=True)  47.2 us
    all_to_all x1, blocking collectives, body(): lax.all_to_all(lax.all_to_all(right_side, 'row', split_axis=2, concat_axi...  32.2 us
    dot_general x6, matrix products, one_block(): jnp.einsum('ihjk,ikhd->ihjd', expo.astype(jnp.bfloat16), value_blk, prefe...  29.8 us
    all_to_all x1, blocking collectives, body(): lax.all_to_all(right_side, 'row', split_axis=2, concat_axis=1, tiled=True)  24 us
    dot_general x6, matrix products, one_block(): jnp.einsum('ijhd,ikhd->ihjk', query_blk, key_blk, preferred_element_type=...  17.9 us
    all_to_all x3, waiting for transfers between devices, from_everyone(): return lax.all_to_all(copies, axis, split_axis=0, concat_axis=0, tiled=True)  16.8 us
  transfers between devices with their start and end apart: 6, of which 6 were waited for; matrix products, arithmetic and copies ran while one was open for 11% of the time, Pallas kernels for 0%

commit v1 on v0

v1 whole, which is shorter than its diff:
```python
import functools
import math

import jax
import jax.numpy as jnp
from jax import lax
from jax.experimental import pallas as pl
from jax.experimental.pallas import tpu as pltpu
from jax.sharding import Mesh
from jax.sharding import PartitionSpec as P

BF = jnp.bfloat16
F32 = jnp.float32
LOG2E = 1.4426950408889634


def layer_norm(values, gain):
    center = values - jnp.mean(values, axis=-1, keepdims=True)
    spread = jnp.mean(center * center, axis=-1, keepdims=True)
    return center * lax.rsqrt(spread + 1e-05) * gain


def dot(a, b):
    return jnp.dot(a, b, preferred_element_type=F32)


def exchange(x, axes):
    return lax.all_to_all(x, axes, split_axis=0, concat_axis=0, tiled=True)


def attention_kernel(
    own_ref, full_ref, two_ref, bias_ref, wq_ref, wkv_ref, wg_ref, wo_ref, out_ref, bias_sc
):
    n_heads, n_q, n_k = bias_sc.shape
    channels = own_ref.shape[-1]
    head = channels // n_heads
    step = 128

    @pl.when(pl.program_id(0) == 0)
    def _():
        for h in range(n_heads):
            bias_sc[h] = bias_ref[h].astype(F32) * LOG2E

    own = own_ref[0]
    q = dot(own, wq_ref[...]).astype(BF)
    kv = dot(full_ref[0], wkv_ref[...]).astype(BF)
    k = kv[:, :channels]
    v = jnp.concatenate([kv[:, channels:], jnp.ones((n_k, channels), BF)], axis=1)
    lane_head = lax.broadcasted_iota(jnp.int32, (step, channels), 1) // head
    scale = LOG2E / math.sqrt(head)
    for t in range(n_q // step):
        rows = slice(t * step, (t + 1) * step)
        acc = jnp.zeros((step, channels), F32)
        for h in range(n_heads):
            mine = lane_head == h
            qm = jnp.where(mine, q[rows], jnp.zeros((), BF))
            s = lax.dot_general(qm, k, (((1,), (1,)), ((), ())), preferred_element_type=F32)
            s = s * scale + bias_sc[h, rows, :]
            top = jnp.max(s, axis=-1, keepdims=True)
            p = jnp.exp2(s - top).astype(BF)
            o = dot(p, v)
            acc = jnp.where(mine, o[:, :channels] / o[:, channels:], acc)
        gate = jax.nn.sigmoid(dot(own[rows], wg_ref[...]))
        gated = (gate * acc).astype(BF)
        res = two_ref[0, rows, :].astype(F32) + dot(gated, wo_ref[...])
        out_ref[0, rows, :] = res.astype(BF)


def attention(own, full, two, bias, wq, wkv, wg, wo):
    n_rows, n_q, channels = own.shape
    n_k = full.shape[1]
    n_heads = bias.shape[0]
    row = lambda i: (i, 0, 0)
    fixed2 = lambda i: (0, 0)
    return pl.pallas_call(
        attention_kernel,
        grid=(n_rows,),
        in_specs=[
            pl.BlockSpec((1, n_q, channels), row),
            pl.BlockSpec((1, n_k, channels), row),
            pl.BlockSpec((1, n_q, channels), row),
            pl.BlockSpec(bias.shape, lambda i: (0, 0, 0)),
            pl.BlockSpec(wq.shape, fixed2),
            pl.BlockSpec(wkv.shape, fixed2),
            pl.BlockSpec(wg.shape, fixed2),
            pl.BlockSpec(wo.shape, fixed2),
        ],
        out_specs=pl.BlockSpec((1, n_q, channels), row),
        out_shape=jax.ShapeDtypeStruct(own.shape, BF),
        scratch_shapes=[pltpu.VMEM((n_heads, n_q, n_k), F32)],
        name="attention",
    )(own, full, two, bias, wq, wkv, wg, wo)


def body(
    pair_in,
    coords,
    chain_ids,
    coord_mask,
    gain_tri,
    gain_sum,
    gain_attn,
    w_tri_in,
    w_tri_out,
    w_bins,
    same_chain,
    w_query,
    w_attn,
    w_bias,
    w_attn_out,
):
    n_rh, n_core, n_col = (lax.axis_size(a) for a in ("rh", "core", "col"))
    rh, core, col = (lax.axis_index(a) for a in ("rh", "core", "col"))
    n_dev = n_rh * n_core * n_col
    every = ("rh", "core", "col")
    row_count, col_count, ch = pair_in.shape
    n_heads = w_bias.shape[1]
    n_bins = w_bins.shape[0]
    sub = row_count // n_col
    half = col_count // n_core
    total = n_rh * n_core * row_count
    n_pa = n_core * sub
    n_q = n_col * half

    moved = exchange(
        pair_in.reshape(sub, n_col, n_core, half, ch)
        .transpose(2, 1, 0, 3, 4)
        .reshape(n_core * n_col, sub, half, ch),
        ("core", "col"),
    )
    pair_c = (
        moved.reshape(n_core, n_col, sub, half, ch).transpose(0, 2, 1, 3, 4).reshape(n_pa, n_q, ch)
    )

    packed = jnp.concatenate(
        [coords, chain_ids.astype(F32)[None], coord_mask.astype(F32)[None]], axis=0
    )
    known = exchange(
        jnp.broadcast_to(packed, (n_rh * n_core, *packed.shape)), ("rh", "core")
    ).reshape(n_rh, n_core, -1, row_count)

    normed = layer_norm(pair_in.astype(F32), gain_tri).astype(BF).reshape(-1, ch)
    proj = dot(normed, w_tri_in[:, : 4 * ch])
    left = (jax.nn.sigmoid(proj[:, :ch]) * proj[:, ch : 2 * ch]).astype(BF)
    right = (jax.nn.sigmoid(proj[:, 2 * ch : 3 * ch]) * proj[:, 3 * ch :]).astype(BF)
    both = jnp.stack([left, right], axis=0).reshape(2, row_count, col_count, ch)
    sides = exchange(both.transpose(3, 0, 1, 2), every).reshape(
        n_rh, n_core, n_col, 2, row_count, col_count
    )
    left_k = sides[:, :, :, 0].transpose(0, 1, 3, 2, 4).reshape(total, total)
    right_k = sides[:, :, :, 1].transpose(1, 0, 3, 2, 4).reshape(total, total)
    product = lax.dot_general(
        left_k, right_k, (((1,), (1,)), ((), ())), preferred_element_type=F32
    ).astype(BF)
    lanes = 128
    n_lt = n_q // lanes
    back = exchange(
        product.reshape(n_rh, n_pa, n_col, n_core, n_lt, lanes)
        .transpose(0, 3, 2, 4, 1, 5)
        .reshape(n_dev, n_lt * n_pa, lanes),
        every,
    )
    product_c = (
        back.reshape(ch, n_lt, n_pa, lanes).transpose(2, 1, 3, 0).reshape(n_pa, n_q, ch).astype(F32)
    )
    summed = layer_norm(product_c, gain_sum).astype(BF)
    wide_c = pair_c.astype(F32)
    normed_c = layer_norm(wide_c, gain_tri).astype(BF).reshape(-1, ch)
    tri_gate = jax.nn.sigmoid(dot(normed_c, w_tri_in[:, 4 * ch :]))
    pair_one = wide_c + (tri_gate * dot(summed.reshape(-1, ch), w_tri_out)).reshape(n_pa, n_q, ch)

    near = lax.dynamic_index_in_dim(known, rh, 0, keepdims=False)
    near = near.transpose(1, 0, 2).reshape(-1, n_core, sub, n_col)
    near = lax.dynamic_index_in_dim(near, col, 3, keepdims=False).reshape(-1, n_pa)
    far = lax.dynamic_index_in_dim(known, core, 1, keepdims=False)
    far = far.transpose(1, 0, 2).reshape(-1, n_q)
    offsets = near[:3, :, None] - far[:3, None, :]
    dist = jnp.sqrt(jnp.sum(offsets * offsets, axis=0) + 1.0)
    centres = 2.0 + 20.0 * jnp.arange(n_bins, dtype=F32) / (n_bins - 1)
    spacing = 25.0 / (n_bins - 1)
    pair_mask = near[4][:, None] * far[4][None, :]
    feats = jnp.exp(-(((dist[..., None] - centres) / spacing) ** 2)) * pair_mask[..., None]
    binned = jnp.dot(feats.reshape(-1, n_bins), w_bins).reshape(n_pa, n_q, ch)
    shared = (near[3][:, None] == far[3][None, :]).astype(F32)
    pair_two = (pair_one + binned + shared[..., None] * same_chain).astype(BF)
    normed_two = layer_norm(pair_two.astype(F32), gain_attn).astype(BF)

    flat_two = normed_two.reshape(-1, ch)
    bias = (
        lax.dot_general(w_bias, flat_two, (((0,), (1,)), ((), ())), preferred_element_type=F32)
        .astype(BF)
        .reshape(n_heads, n_core, sub, n_q)
        .transpose(1, 0, 2, 3)
        .reshape(n_core, n_heads * sub, n_q)
    )
    spread = exchange(
        jnp.broadcast_to(
            bias[None, :, None], (n_rh, n_core, n_col, n_heads * sub, n_q)
        ).reshape(n_dev, n_heads * sub, n_q),
        every,
    )
    bias_c = (
        spread.reshape(n_rh, n_core, n_col, n_heads, sub, n_q)
        .transpose(3, 0, 4, 2, 1, 5)
        .reshape(n_heads, n_q, n_core * n_q)
    )

    order = [(d, d ^ n_col) for d in range(n_dev)]
    other = lax.ppermute(normed_two, every, order)
    full = jnp.where(
        core == 0,
        jnp.concatenate([normed_two, other], axis=1),
        jnp.concatenate([other, normed_two], axis=1),
    )
    result = attention(
        normed_two,
        full,
        pair_two,
        bias_c,
        w_query,
        w_attn[:, : 2 * ch],
        w_attn[:, 2 * ch :],
        w_attn_out,
    )
    home = exchange(
        result.reshape(n_core, sub, n_col, half, ch)
        .transpose(0, 2, 1, 3, 4)
        .reshape(n_core * n_col, sub, half, ch),
        ("core", "col"),
    )
    return (
        home.reshape(n_core, n_col, sub, half, ch)
        .transpose(2, 1, 0, 3, 4)
        .reshape(row_count, col_count, ch)
    )


def solution(mesh):
    n_row, n_col = mesh.shape["row"], mesh.shape["col"]
    split = Mesh(mesh.devices.reshape(n_row // 2, 2, n_col), ("rh", "core", "col"))
    row = ("rh", "core")
    return jax.shard_map(
        body,
        mesh=split,
        in_specs=(P(row, "col", None), P(None, row), P(row), P(row)) + (P(),) * 11,
        out_specs=P(row, "col", None),
        check_vma=False,
    )
```

time: 549 us -> 273 us (0.50); the launches traced: 541 us -> 272 us
  waiting for transfers between devices: 223 us -> 84.5 us
  matrix products: 85.4 us -> 12.9 us
  blocking collectives: 92.6 us -> 23.2 us
  Pallas kernels: 0 us -> 41 us
  local copies, waits for them, and re-layouts: 79.8 us -> 40.7 us
  starting transfers between devices: 13.6 us -> 35.2 us
  between operations: 14.1 us -> 0.52 us
    all_gather x3 -> x0, waiting for transfers between devices: 206 us -> none  [the longest x1 93.9 us: body(): lax.all_gather(moved, 'row', axis=2, tiled=True)]
    dot_general x20 -> x6, matrix products: 85.4 us -> 12.9 us  [the longest x3 7.64 us: dot(): return jnp.dot(a, b, preferred_element_type=F32)]
    all_to_all x5 -> x1, blocking collectives: 92.6 us -> 23.2 us  [exchange(): return lax.all_to_all(x, axes, split_axis=0, concat_axis=0, tiled=True)]
    all_to_all x3 -> x5, waiting for transfers between devices: 16.8 us -> 83.2 us  [exchange(): return lax.all_to_all(x, axes, split_axis=0, concat_axis=0, tiled=True)]
    pallas_call x0 -> x1, Pallas kernels: none -> 41 us  [attention(): pl.pallas_call(attention_kernel, grid=(n_rows,), in_specs=[pl.BlockSpec((...]
    all_to_all x3 -> x5, starting transfers between devices: 13.3 us -> 33.8 us  [exchange(): return lax.all_to_all(x, axes, split_axis=0, concat_axis=0, tiled=True)]
    reduce_sum x6 -> x0, other arithmetic: 14.5 us -> none  [one_block(): new_total = running_total * rescale + jnp.sum(expo, axis=-1)]
    convert_element_type x6 -> x8, other arithmetic: 3.54 us -> 17.9 us  [the longest x1 6.42 us: body(): left = (jax.nn.sigmoid(proj[:, :ch]) * proj[:, ch:2 * ch]).astype(BF)]
  transfers between devices with their start and end apart: 6 -> 6, of which waited for: 6 -> 5; matrix products, arithmetic and copies ran while one was open for 11% -> 15% of each run, Pallas kernels for 0% -> 0%
where the time goes in v1:
time: 273 us; the launch traced here: 272 us
  waiting for transfers between devices  84.5 us (31%)
  Pallas kernels  41 us (15%)
  local copies, waits for them, and re-layouts  40.7 us (15%)
  starting transfers between devices  35.2 us (13%)
  other arithmetic  34.3 us (13%)
  blocking collectives  23.2 us (8%)
  matrix products  12.9 us (5%)
    all_to_all x5, waiting for transfers between devices, exchange(): return lax.all_to_all(x, axes, split_axis=0, concat_axis=0, tiled=True)  83.2 us
    pallas_call x1, Pallas kernels, attention(): pl.pallas_call(attention_kernel, grid=(n_rows,), in_specs=[pl.BlockSpec((...  41 us
    all_to_all x5, starting transfers between devices, exchange(): return lax.all_to_all(x, axes, split_axis=0, concat_axis=0, tiled=True)  33.8 us
    all_to_all x1, blocking collectives, exchange(): return lax.all_to_all(x, axes, split_axis=0, concat_axis=0, tiled=True)  23.2 us
    dot_general x3, matrix products, dot(): return jnp.dot(a, b, preferred_element_type=F32)  7.64 us
    transpose x2, local copies, waits for them, and re-layouts, body(): right_k = sides[:, :, :, 1].transpose(1, 0, 3, 2, 4).reshape(total, total)  6.69 us
    convert_element_type x1, other arithmetic, body(): left = (jax.nn.sigmoid(proj[:, :ch]) * proj[:, ch:2 * ch]).astype(BF)  6.42 us
    reduce_sum x4, other arithmetic, layer_norm(): spread = jnp.mean(center * center, axis=-1, keepdims=True)  5.99 us
  transfers between devices with their start and end apart: 6, of which 5 were waited for; matrix products, arithmetic and copies ran while one was open for 15% of the time, Pallas kernels for 0%

profile of v1, /device:TPU:1, one launch (start us, length us, event | category | flops | bytes accessed | tf_op | source)
XLA Modules:
  0.0 272.3 jit_solution(10979887518687862393)
XLA Ops:
  0.0 0.8 convert_bitcast_fusion.2
  0.8 0.7 pad_maximum_fusion
  1.5 0.7 reshape.329
  2.2 6.8 %all-to-all-start.3 = ((f32[16,1,240]{2,1,0:T(1,128)}), f32[16,1,240]{2,1,0:T(1,128)S(1)}, u32[]{:S(2)}, u32[]{:S(2)}) async-start(f32[16,1,240]{2,1,0:T(1,128)} %reshape.329), calls=%async_computation.3 | async-start | bytes 32768 | tf_op jit(solution)/shard_map/all_to_all | solution.py:28
  9.0 1.8 convert_reduce_fusion.1
  10.8 2.7 fusion.11
  13.6 1.5 fusion.13
  15.0 5.0 %fusion.40 = f32[4608,512]{1,0:T(8,128)} fusion(bf16[4608,128]{1,0:T(8,128)(2,1)S(1)} %bitcast.127, bf16[128,640]{1,0:T(8,128)(2,1)S(1)} %copy-done.5), kind=kOutput, calls=%fused_computation.63 | convolution fusion | flops 603979776 | bytes 10747904 | tf_op jit(solution)/shard_map/dot_general | solution.py:24
  20.0 1.1 copy.65
  21.1 7.8 %all-to-all-start = ((bf16[16,6,48,128]{3,2,1,0:T(8,128)(2,1)}), bf16[16,6,48,128]{3,2,1,0:T(8,128)(2,1)S(1)}, u32[]{:S(2)}, u32[]{:S(2)}) async-start(bf16[16,6,48,128]{3,2,1,0:T(8,128)(2,1)} %bitcast.2), calls=%async_computation | async-start | bytes 2359296 | tf_op jit(solution)/shard_map/all_to_all | solution.py:28
  28.9 6.4 %fusion.18 = (bf16[4608,128]{1,0:T(8,128)(2,1)}, bf16[4608,128]{1,0:T(8,128)(2,1)}) fusion(f32[4608,512]{1,0:T(8,128)} %fusion.40), kind=kLoop, calls=%fused_computation.29 | loop fusion | flops 5898240 | bytes 11796480 | tf_op jit(solution)/shard_map/convert_element_type | solution.py:144
  35.3 2.0 copy.70
  37.3 2.7 copy.71
  40.0 3.7 %maximum_bitcast_fusion = bf16[128,2,48,96]{3,2,1,0:T(8,128)(2,1)} fusion(bf16[1,48,96,128]{2,1,0,3:T(8,128)(2,1)} %copy.71, bf16[1,48,96,128]{2,1,0,3:T(8,128)(2,1)S(1)} %copy.70), kind=kLoop, calls=%fused_computation.7 | loop fusion | flops 1179648 | bytes 4718592 | tf_op jit(solution)/shard_map/transpose | solution.py:147
  43.7 0.5 broadcast.198
  44.2 0.6 reduce.10
  44.9 3.1 %all-to-all-done = bf16[16,6,48,128]{3,2,1,0:T(8,128)(2,1)S(1)} async-done(((bf16[16,6,48,128]{3,2,1,0:T(8,128)(2,1)}), bf16[16,6,48,128]{3,2,1,0:T(8,128)(2,1)S(1)}, u32[]{:S(2)}, u32[]{:S(2)}) %all-to-all-start) | async-done | bytes 1179680 | tf_op jit(solution)/shard_map/all_to_all | solution.py:28
  48.0 7.0 %all-to-all-start.1 = ((bf16[128,2,48,96]{3,2,1,0:T(8,128)(2,1)}), bf16[128,2,48,96]{3,2,1,0:T(8,128)(2,1)}, u32[]{:S(2)}, u32[]{:S(2)}) async-start(bf16[128,2,48,96]{3,2,1,0:T(8,128)(2,1)} %maximum_bitcast_fusion), calls=%async_computation.1 | async-start | bytes 6291456 | tf_op jit(solution)/shard_map/all_to_all | solution.py:28
  55.1 0.2 dynamic-slice_reduce_fusion.2
  55.6 0.2 dynamic-slice_reduce_fusion
  55.7 0.1 sub.86
  56.2 0.7 fusion.28
  56.9 1.4 multiply_reduce_fusion.1
  58.6 0.2 convert_bitcast_fusion.1
  58.8 0.2 copy.66
  59.0 36.6 %all-to-all-done.1 = bf16[128,2,48,96]{3,2,1,0:T(8,128)(2,1)} async-done(((bf16[128,2,48,96]{3,2,1,0:T(8,128)(2,1)}), bf16[128,2,48,96]{3,2,1,0:T(8,128)(2,1)}, u32[]{:S(2)}, u32[]{:S(2)}) %all-to-all-start.1) | async-done | bytes 2359328 | tf_op jit(solution)/shard_map/all_to_all | solution.py:28
  95.6 3.7 %slice_bitcast_fusion = (bf16[2,8,48,8,96]{4,2,3,0,1:T(8,128)(2,1)}, bf16[8,2,48,8,96]{4,2,3,1,0:T(8,128)(2,1)S(1)}) fusion(bf16[8,2,8,2,48,96]{5,4,3,2,1,0:T(8,128)(2,1)} %bitcast.12), kind=kLoop, calls=%fused_computation.48 | loop fusion | bytes 4718592 | tf_op jit(solution)/shard_map/transpose | solution.py:151
  99.3 1.6 copy.72
  100.9 3.8 %reshape.301 = bf16[768,768]{1,0:T(8,128)(2,1)} reshape(bf16[8,2,48,8,96]{4,3,2,1,0:T(8,128)(2,1)} %copy.72) | data formatting | bytes 2359296 | tf_op jit(solution)/shard_map/reshape | solution.py:150
  104.7 3.0 %copy.73 = bf16[2,8,48,8,96]{4,3,2,1,0:T(8,128)(2,1)} copy(bf16[2,8,48,8,96]{4,2,3,0,1:T(8,128)(2,1)} %get-tuple-element.9) | data formatting | bytes 2359296 | tf_op jit(solution)/shard_map/transpose | solution.py:151
  107.7 3.8 %reshape.302 = bf16[768,768]{1,0:T(8,128)(2,1)} reshape(bf16[2,8,48,8,96]{4,3,2,1,0:T(8,128)(2,1)} %copy.73) | data formatting | bytes 2359296 | tf_op jit(solution)/shard_map/reshape | solution.py:151
  111.4 2.7 %convolution_convert_fusion.1 = bf16[768,768]{1,0:T(8,128)(2,1)S(1)} fusion(bf16[768,768]{1,0:T(8,128)(2,1)} %reshape.301, bf16[768,768]{1,0:T(8,128)(2,1)} %reshape.302), kind=kOutput, calls=%fused_computation.50 | convolution fusion | flops 906559488 | bytes 3538944 | tf_op jit(solution)/shard_map/dot_general | solution.py:152
  114.2 0.3 copy.74
  114.5 1.9 copy.75
  116.4 6.2 %all-to-all-start.2 = ((bf16[128,36,128]{2,1,0:T(8,128)(2,1)}), bf16[128,36,128]{2,1,0:T(8,128)(2,1)}, u32[]{:S(2)}, u32[]{:S(2)}) async-start(bf16[128,36,128]{2,1,0:T(8,128)(2,1)} %copy.75), calls=%async_computation.2 | async-start | bytes 2621440 | tf_op jit(solution)/shard_map/all_to_all | solution.py:28
  122.5 2.5 fusion.27
  125.1 2.2 fusion.2
  127.3 16.6 %all-to-all-done.2 = bf16[128,36,128]{2,1,0:T(8,128)(2,1)} async-done(((bf16[128,36,128]{2,1,0:T(8,128)(2,1)}), bf16[128,36,128]{2,1,0:T(8,128)(2,1)}, u32[]{:S(2)}, u32[]{:S(2)}) %all-to-all-start.2) | async-done | bytes 1179680 | tf_op jit(solution)/shard_map/all_to_all | solution.py:28
  143.9 1.6 copy.76
  145.5 0.2 fusion.29
  145.8 0.4 multiply_reduce_fusion
  146.2 1.7 convert_bitcast_fusion
  147.9 3.1 %copy.77 = f32[12,3,128,128]{3,2,1,0:T(8,128)} copy(f32[12,3,128,128]{2,3,0,1:T(8,128)} %convert_bitcast_fusion) | data formatting | bytes 4718592 | tf_op jit(solution)/shard_map/convert_element_type | solution.py:164
  151.0 4.1 %fusion.24 = bf16[4608,128]{1,0:T(8,128)(2,1)S(1)} fusion(f32[12,3,128,128]{3,2,1,0:T(8,128)} %copy.77, f32[128]{0:T(128)S(1)} %copy-done.12, f32[4608]{0:T(1024)S(1)} %rsqrt.42, f32[4608]{0:T(1024)S(1)} %div.58), kind=kLoop, calls=%fused_computation.39 | loop fusion | flops 2359296 | bytes 3576320 | tf_op jit(solution)/shard_map/convert_element_type | solution.py:166
  155.2 0.5 convolution_multiply_fusion
  155.6 0.2 copy-done.7
  155.9 2.1 convert_reduce_fusion
  158.1 1.4 fusion.8
  159.6 1.5 fusion.10.own_ref
  161.1 0.4 fusion.3
  161.6 1.8 broadcast_in_dim.14
  163.3 6.1 %all-to-all-start.4 = ((bf16[128,24,384]{2,1,0:T(8,128)(2,1)}), bf16[128,24,384]{2,1,0:T(8,128)(2,1)}, u32[]{:S(2)}, u32[]{:S(2)}) async-start(bf16[128,24,384]{2,1,0:T(8,128)(2,1)} %bitcast.123), calls=%async_computation.4 | async-start | bytes 4718592 | tf_op jit(solution)/shard_map/all_to_all | solution.py:28
  169.4 1.4 collective-permute-start
  170.8 0.6 slice.68.wkv_ref
  171.4 0.6 slice.69.wg_ref
  172.0 1.2 collective-permute-done
  173.3 1.7 maximum_select_fusion.full_ref
  175.0 26.9 %all-to-all-done.4 = bf16[128,24,384]{2,1,0:T(8,128)(2,1)} async-done(((bf16[128,24,384]{2,1,0:T(8,128)(2,1)}), bf16[128,24,384]{2,1,0:T(8,128)(2,1)}, u32[]{:S(2)}, u32[]{:S(2)}) %all-to-all-start.4) | async-done | bytes 2359328 | tf_op jit(solution)/shard_map/all_to_all | solution.py:28
  201.9 2.1 copy.83
  204.0 1.7 copy.84
  205.6 41.0 %attention.1 = bf16[12,384,128]{2,1,0:T(8,128)(2,1)} custom-call(bf16[12,384,128]{2,1,0:T(8,128)(2,1)} %copy-done.2, bf16[12,768,128]{2,1,0:T(8,128)(2,1)} %maximum_select_fusion.full_ref, bf16[12,384,128]{2,1,0:T(8,128)(2,1)} %copy-done.3, bf16[4,384,768]{2,1,0:T(8,128)(2,1)} %bitcast.125, bf16[128,128]{1,0:T(8,128)(2,1)} %wq_ref.1, ...), custom_call_target="tpu_custom_call" | custom-call | tf_op jit(solution)/shard_map/attention/pallas_call | solution.py:75
  246.6 1.3 copy.85
  248.0 23.2 %all_to_all.30 = bf16[16,6,48,128]{3,2,1,0:T(8,128)(2,1)S(1)} all-to-all(bf16[16,6,48,128]{3,2,1,0:T(8,128)(2,1)S(1)} %bitcast.131), channel_id=1, replica_groups=mesh['rh'=8,'core'=2,'col'=8] {'core','col'}, dimensions={0} | all-to-all | bytes 2359296 | tf_op jit(solution)/shard_map/all_to_all | solution.py:28
  271.2 1.1 copy.86
  (63 shorter events, 1.3 us)
Async XLA Ops:
  0.0 155.1 %copy-start = (bf16[128,128]{1,0:T(8,128)(2,1)S(1)}, bf16[128,128]{1,0:T(8,128)(2,1)}, u32[]{:S(2)}) copy-start(bf16[128,128]{1,0:T(8,128)(2,1)} %param.23) | copy-start | bytes 98308
  0.0 13.5 %copy-start.1 = (bf16[48,96,128]{2,1,0:T(8,128)(2,1)S(1)}, bf16[48,96,128]{2,1,0:T(8,128)(2,1)}, u32[]{:S(2)}) copy-start(bf16[48,96,128]{2,1,0:T(8,128)(2,1)} %param.15) | copy-start | bytes 3538948
  0.0 13.5 %copy-start.8 = (f32[128]{0:T(128)S(1)}, f32[128]{0:T(128)}, u32[]{:S(2)}) copy-start(f32[128]{0:T(128)} %param.19) | copy-start | bytes 1540
  2.2 18.9 %all-to-all-start.3 = ((f32[16,1,240]{2,1,0:T(1,128)}), f32[16,1,240]{2,1,0:T(1,128)S(1)}, u32[]{:S(2)}, u32[]{:S(2)}) async-start(f32[16,1,240]{2,1,0:T(1,128)} %reshape.329), calls=%async_computation.3 | async-start | bytes 32768 | tf_op jit(solution)/shard_map/all_to_all | solution.py:28
  9.0 6.0 %copy-start.5 = (bf16[128,640]{1,0:T(8,128)(2,1)S(1)}, bf16[128,640]{1,0:T(8,128)(2,1)}, u32[]{:S(2)}) copy-start(bf16[128,640]{1,0:T(8,128)(2,1)} %param.22) | copy-start | bytes 491524
  21.1 26.8 %all-to-all-start = ((bf16[16,6,48,128]{3,2,1,0:T(8,128)(2,1)}), bf16[16,6,48,128]{3,2,1,0:T(8,128)(2,1)S(1)}, u32[]{:S(2)}, u32[]{:S(2)}) async-start(bf16[16,6,48,128]{3,2,1,0:T(8,128)(2,1)} %bitcast.2), calls=%async_computation | async-start | bytes 2359296 | tf_op jit(solution)/shard_map/all_to_all | solution.py:28
  48.0 47.7 %all-to-all-start.1 = ((bf16[128,2,48,96]{3,2,1,0:T(8,128)(2,1)}), bf16[128,2,48,96]{3,2,1,0:T(8,128)(2,1)}, u32[]{:S(2)}, u32[]{:S(2)}) async-start(bf16[128,2,48,96]{3,2,1,0:T(8,128)(2,1)} %maximum_bitcast_fusion), calls=%async_computation.1 | async-start | bytes 6291456 | tf_op jit(solution)/shard_map/all_to_all | solution.py:28
  116.4 27.5 %all-to-all-start.2 = ((bf16[128,36,128]{2,1,0:T(8,128)(2,1)}), bf16[128,36,128]{2,1,0:T(8,128)(2,1)}, u32[]{:S(2)}, u32[]{:S(2)}) async-start(bf16[128,36,128]{2,1,0:T(8,128)(2,1)} %copy.75), calls=%async_computation.2 | async-start | bytes 2621440 | tf_op jit(solution)/shard_map/all_to_all | solution.py:28
  147.9 3.1 %copy-start.12 = (f32[128]{0:T(128)S(1)}, f32[128]{0:T(128)}, u32[]{:S(2)}) copy-start(f32[128]{0:T(128)} %param.20) | copy-start | bytes 1540
  151.0 4.1 %copy-start.4 = (f32[4608,128]{1,0:T(8,128)S(1)}, f32[4608,128]{1,0:T(8,128)}, u32[]{:S(2)}) copy-start(f32[4608,128]{1,0:T(8,128)} %fusion.2) | copy-start | bytes 7077892
  155.2 0.7 copy-start.7
  155.2 0.7 copy-start.10
  155.9 3.7 %copy-start.11 = (f32[128]{0:T(128)S(1)}, f32[128]{0:T(128)}, u32[]{:S(2)}) copy-start(f32[128]{0:T(128)} %param.21) | copy-start | bytes 1540
  158.0 1.5 copy-start.3
  158.1 3.0 %copy-start.9 = (bf16[128,4]{0,1:T(4,128)(2,1)S(1)}, bf16[128,4]{0,1:T(4,128)(2,1)}, u32[]{:S(2)}) copy-start(bf16[128,4]{0,1:T(4,128)(2,1)} %param.28) | copy-start | bytes 3076
  161.0 12.2 %copy-start.2 = (bf16[12,384,128]{2,1,0:T(8,128)(2,1)}, bf16[12,384,128]{2,1,0:T(8,128)(2,1)S(1)}, u32[]{:S(2)}) copy-start(bf16[12,384,128]{2,1,0:T(8,128)(2,1)S(1)} %fusion.10.own_ref) | copy-start | bytes 3538948
  163.3 7.4 %copy-start.6 = (bf16[128,384]{1,0:T(8,128)(2,1)S(1)}, bf16[128,384]{1,0:T(8,128)(2,1)}, u32[]{:S(2)}) copy-start(bf16[128,384]{1,0:T(8,128)(2,1)} %param.27) | copy-start | bytes 294916
  163.3 38.5 %all-to-all-start.4 = ((bf16[128,24,384]{2,1,0:T(8,128)(2,1)}), bf16[128,24,384]{2,1,0:T(8,128)(2,1)}, u32[]{:S(2)}, u32[]{:S(2)}) async-start(bf16[128,24,384]{2,1,0:T(8,128)(2,1)} %bitcast.123), calls=%async_computation.4 | async-start | bytes 4718592 | tf_op jit(solution)/shard_map/all_to_all | solution.py:28
  169.4 3.8 %collective-permute-start = (bf16[12,384,128]{2,1,0:T(8,128)(2,1)S(1)}, bf16[12,384,128]{2,1,0:T(8,128)(2,1)S(1)}, u32[]{:S(2)}, u32[]{:S(2)}) collective-permute-start(bf16[12,384,128]{2,1,0:T(8,128)(2,1)S(1)} %fusion.10.own_ref), channel_id=1, source_target_pairs={{0,8},{1,9},{2,10},{3,11},{4,12},{5,13},{6,14},{7,15},{8,0},{9,1},... | collective-permute-start | bytes 3538952 | tf_op jit(solution)/shard_map/ppermute | solution.py:209

commit v2 on v1

v2 whole, which is shorter than its diff:
```python
import functools
import math

import jax
import jax.numpy as jnp
from jax import lax
from jax.experimental import pallas as pl
from jax.experimental.pallas import tpu as pltpu
from jax.sharding import Mesh
from jax.sharding import PartitionSpec as P

BF = jnp.bfloat16
F32 = jnp.float32
LOG2E = 1.4426950408889634
NT = (((1,), (1,)), ((), ()))
LANES = 128


def layer_norm(values, gain):
    center = values - jnp.mean(values, axis=-1, keepdims=True)
    spread = jnp.mean(center * center, axis=-1, keepdims=True)
    return center * lax.rsqrt(spread + 1e-05) * gain


def dot(a, b):
    return jnp.dot(a, b, preferred_element_type=F32)


def dot_nt(a, b):
    return lax.dot_general(a, b, NT, preferred_element_type=F32)


def exchange(x, axes):
    return lax.all_to_all(x, axes, split_axis=0, concat_axis=0, tiled=True)


def sides_kernel(x_ref, gain_ref, w_ref, out_ref, norm_sc, sc):
    n_rows, n_cols, ch = x_ref.shape
    n_out = out_ref.shape[1]
    third = n_rows // 3
    cut = LANES - n_cols

    def norm(i, carry):
        for u in range(4):
            norm_sc[i * 4 + u] = layer_norm(x_ref[i * 4 + u].astype(F32), gain_ref[...]).astype(BF)
        return carry

    lax.fori_loop(0, n_rows // 4, norm, 0)

    def sides(x):
        pr = dot_nt(w_ref[...], x)
        left = jax.nn.sigmoid(pr[:ch]) * pr[ch : 2 * ch]
        right = jax.nn.sigmoid(pr[2 * ch : 3 * ch]) * pr[3 * ch :]
        return left, right

    def put(row, value):
        sc[pl.ds(row, ch, stride=n_out), :] = value

    def main(s, carry):
        x = jnp.concatenate(
            [
                norm_sc[s],
                norm_sc[third + s, :cut],
                norm_sc[2 * third + s],
                norm_sc[third + s, cut : 2 * cut],
            ],
            axis=0,
        )
        left, right = sides(x)
        put(s, left[:, :LANES])
        put(third + s, left[:, LANES:])
        put(2 * third + s, right[:, :LANES])
        put(3 * third + s, right[:, LANES:])
        return carry

    lax.fori_loop(0, third, main, 0)

    is_left = lax.broadcasted_iota(jnp.int32, (ch, LANES), 1) < LANES // 2

    def rest(s, carry):
        one = norm_sc[third + s, 2 * cut :]
        two = norm_sc[third + third // 2 + s, 2 * cut :]
        left, right = sides(jnp.concatenate([one, two, one, two], axis=0))
        put(4 * third + s, jnp.where(is_left, left, right))
        return carry

    lax.fori_loop(0, third // 2, rest, 0)

    def emit(c, carry):
        out_ref[c] = sc[pl.ds(pl.multiple_of(c * n_out, 8), n_out), :].astype(BF)
        return carry

    lax.fori_loop(0, ch, emit, 0)


def make_sides(pair, gain, w_t):
    n_rows, n_cols, ch = pair.shape
    n_out = 2 * n_rows * n_cols // LANES
    return pl.pallas_call(
        sides_kernel,
        out_shape=jax.ShapeDtypeStruct((ch, n_out, LANES), BF),
        scratch_shapes=[
            pltpu.VMEM(pair.shape, BF),
            pltpu.VMEM((ch * n_out, LANES), F32),
        ],
        name="sides",
    )(pair, gain.reshape(1, ch), w_t)


def triangle_kernel(n_rh, n_core, n_col, n_rows, n_cols, in_ref, out_ref, l_sc, r_sc, p_sc):
    third = n_rows // 3
    cut = LANES - n_cols
    total = n_rh * n_core * n_rows
    n_pa = n_core * n_rows // n_col
    n_lt = total // n_core // LANES
    lane = lax.broadcasted_iota(jnp.int32, (third, LANES), 1)

    def middle(a, b, c):
        return jnp.where(
            lane < cut,
            pltpu.roll(a, cut, 1),
            jnp.where(lane < 2 * cut, pltpu.roll(b, 2 * cut, 1), jnp.where(lane < n_cols, c, 0.0)),
        )

    def unpack(rh, carry):
        for p in range(n_core):
            for c in range(n_col):
                blk = in_ref[(rh * n_core + p) * n_col + c].astype(F32)
                b = [blk[third * t : third * (t + 1)] for t in range(4)]
                last = blk[4 * third :]
                keep = [jnp.where(lane < n_cols, t, 0.0) for t in b]
                lc = jnp.concatenate([pltpu.roll(last, 2 * cut, 1), pltpu.roll(last, cut, 1)], axis=0)
                rc = jnp.concatenate([last, pltpu.roll(last, 3 * cut, 1)], axis=0)
                left = jnp.concatenate([keep[0], middle(b[0], b[1], lc), keep[1]], axis=0)
                right = jnp.concatenate([keep[2], middle(b[2], b[3], rc), keep[3]], axis=0)
                lanes = slice(c * LANES, (c + 1) * LANES)
                at_l = pl.multiple_of((rh * n_core + p) * n_rows, 16)
                at_r = pl.multiple_of((p * n_rh + rh) * n_rows, 16)
                l_sc[pl.ds(at_l, n_rows), lanes] = left.astype(BF)
                r_sc[pl.ds(at_r, n_rows), lanes] = right.astype(BF)
        return carry

    lax.fori_loop(0, n_rh, unpack, 0)
    wide = 2 * LANES
    for t in range(total // wide):
        part = dot_nt(l_sc[...], r_sc[t * wide : (t + 1) * wide, :])
        p_sc[2 * t] = part[:, :LANES]
        p_sc[2 * t + 1] = part[:, LANES:]

    def pack(rh, carry):
        for core in range(n_core):
            for c in range(n_col):
                rows = pl.ds(rh * n_core * n_rows + c, n_pa, stride=n_col)
                parts = [p_sc[core * n_lt + t, rows, :] for t in range(n_lt)]
                out_ref[(rh * n_core + core) * n_col + c] = jnp.concatenate(parts, axis=0).astype(BF)
        return carry

    lax.fori_loop(0, n_rh, pack, 0)


def triangle(sides, n_rh, n_core, n_col, n_rows, n_cols):
    total = n_rh * n_core * n_rows
    n_pa = n_core * n_rows // n_col
    n_lt = total // n_core // LANES
    return pl.pallas_call(
        functools.partial(triangle_kernel, n_rh, n_core, n_col, n_rows, n_cols),
        out_shape=jax.ShapeDtypeStruct((sides.shape[0], n_lt * n_pa, LANES), BF),
        scratch_shapes=[
            pltpu.VMEM((total, n_col * LANES), BF),
            pltpu.VMEM((total, n_col * LANES), BF),
            pltpu.VMEM((total // LANES, total, LANES), F32),
        ],
        name="triangle",
    )(sides)


def update_kernel(
    n_bins,
    back_ref,
    pair_ref,
    near_ref,
    far_ref,
    gain_tri_ref,
    gain_sum_ref,
    gain_attn_ref,
    wgo_ref,
    wout_ref,
    wbins_ref,
    same_ref,
    wbias_ref,
    two_ref,
    normed_ref,
    bias_ref,
    sc,
):
    ch, n_in, _ = back_ref.shape
    n_q = far_ref.shape[0]
    n_lt = n_q // LANES
    n_pa = n_in // n_lt
    n_in8 = sc.shape[0] // ch
    sub = pair_ref.shape[2]
    pa = pl.program_id(0)
    n_heads = bias_ref.shape[1]

    @pl.when(pa == 0)
    def _():
        def widen(c, carry):
            sc[pl.ds(pl.multiple_of(c * n_in8, 8), n_in), :] = back_ref[c].astype(F32)
            return carry

        lax.fori_loop(0, ch, widen, 0)

    parts = []
    for t in range(n_lt):
        x = sc[pl.ds(t * n_pa + pa, ch, stride=n_in8), :]
        center = x - jnp.mean(x, axis=0, keepdims=True)
        spread = jnp.mean(center * center, axis=0, keepdims=True)
        summed = (center * lax.rsqrt(spread + 1e-05) * gain_sum_ref[...]).astype(BF)
        parts.append(
            lax.dot_general(
                summed, wout_ref[...], (((0,), (0,)), ((), ())), preferred_element_type=F32
            )
        )
    tri = jnp.concatenate(parts, axis=0)
    wide = pair_ref[0, :, 0].reshape(n_q, ch).astype(F32)
    gate = jax.nn.sigmoid(dot(layer_norm(wide, gain_tri_ref[...]).astype(BF), wgo_ref[...]))
    far = far_ref[...]
    near = [near_ref[f, pa] for f in range(5)]
    square = jnp.zeros((n_q, 1), F32)
    for f in range(3):
        off = far[:, f : f + 1] - near[f]
        square = square + off * off
    dist = jnp.sqrt(square + 1.0)
    bins = lax.broadcasted_iota(jnp.int32, (1, ch), 1).astype(F32)
    centres = 2.0 + 20.0 * bins / (n_bins - 1)
    z = (dist - centres) * ((n_bins - 1) / 25.0)
    feats = jnp.exp(-(z * z)) * (far[:, 4:5] * near[4])
    binned = dot(feats, wbins_ref[...])
    shared = (far[:, 3:4] == near[3]).astype(F32)
    two = (wide + gate * tri + binned + shared * same_ref[...]).astype(BF)
    two_ref[0] = two
    normed = layer_norm(two.astype(F32), gain_attn_ref[...]).astype(BF)
    normed_ref[0] = normed
    bias_ref[0] = dot_nt(wbias_ref[...], normed)[:n_heads].astype(BF)


def update(back, moved, near, far, gains, wgo, wout, wbins, same, wbias_t, n_heads, n_bins):
    ch, n_in, _ = back.shape
    n_core, n_col, sub, half, _ = moved.shape
    n_q = n_col * half
    n_pa = n_core * sub
    n_in8 = -(-n_in // 8) * 8
    fixed = lambda i: (0, 0)
    row = lambda i: (i, 0, 0)
    return pl.pallas_call(
        functools.partial(update_kernel, n_bins),
        grid=(n_pa,),
        in_specs=[
            pl.BlockSpec(back.shape, lambda i: (0, 0, 0)),
            pl.BlockSpec((1, n_col, 1, half, ch), lambda i: (i // sub, 0, i % sub, 0, 0)),
            pl.BlockSpec(memory_space=pltpu.SMEM),
            pl.BlockSpec(far.shape, fixed),
            pl.BlockSpec((1, ch), fixed),
            pl.BlockSpec((ch, 1), fixed),
            pl.BlockSpec((1, ch), fixed),
            pl.BlockSpec(wgo.shape, fixed),
            pl.BlockSpec(wout.shape, fixed),
            pl.BlockSpec(wbins.shape, fixed),
            pl.BlockSpec(same.shape, fixed),
            pl.BlockSpec(wbias_t.shape, fixed),
        ],
        out_specs=[
            pl.BlockSpec((1, n_q, ch), row),
            pl.BlockSpec((1, n_q, ch), row),
            pl.BlockSpec((1, n_heads, n_q), row),
        ],
        out_shape=[
            jax.ShapeDtypeStruct((n_pa, n_q, ch), BF),
            jax.ShapeDtypeStruct((n_pa, n_q, ch), BF),
            jax.ShapeDtypeStruct((n_pa, n_heads, n_q), BF),
        ],
        scratch_shapes=[pltpu.VMEM((ch * n_in8, LANES), F32)],
        name="update",
    )(back, moved, near, far, gains[0], gains[1], gains[2], wgo, wout, wbins, same, wbias_t)


def attention_kernel(
    core_ref,
    own_ref,
    other_ref,
    two_ref,
    bias_ref,
    wq_ref,
    wkv_ref,
    wg_ref,
    wo_ref,
    out_ref,
    raw_sc,
    bias_sc,
    kv_sc,
):
    n_lt, tall, n_k = bias_sc.shape
    n_q, channels = own_ref.shape[1:]
    n_heads = tall // LANES
    n_src, n_pay, _ = bias_ref.shape
    sub = n_pay // n_heads
    n_col = n_q // sub // (n_src // 16)
    head = channels // n_heads

    @pl.when(pl.program_id(0) == 0)
    def _():
        def widen(d, carry):
            for t in range(n_lt):
                part = bias_ref[d, :, t * LANES : (t + 1) * LANES]
                raw_sc[t, pl.ds(pl.multiple_of(d * n_pay, 8), n_pay), :] = part.astype(F32) * LOG2E
            return carry

        lax.fori_loop(0, n_src, widen, 0)
        n_rh = n_src // 2 // n_col
        for rh in range(n_rh):
            for a in range(sub):
                q0 = rh * sub * n_col + a * n_col
                t, q1 = q0 // LANES, q0 % LANES
                for s in range(2):
                    for h in range(n_heads):
                        for u in range(n_lt):
                            at = (rh * 2 + s) * n_col * n_pay + a * n_heads + h
                            bias_sc[
                                t,
                                h * LANES + q1 : h * LANES + q1 + n_col,
                                s * n_q + u * LANES : s * n_q + (u + 1) * LANES,
                            ] = raw_sc[u, pl.ds(at, n_col, stride=n_pay), :]

    core = core_ref[0]
    own = own_ref[0]
    q = dot(own, wq_ref[...]).astype(BF)
    kv_sc[pl.ds(pl.multiple_of(core * n_q, LANES), n_q), : 2 * channels] = dot(
        own, wkv_ref[...]
    ).astype(BF)
    kv_sc[pl.ds(pl.multiple_of((1 - core) * n_q, LANES), n_q), : 2 * channels] = dot(
        other_ref[0], wkv_ref[...]
    ).astype(BF)
    kv_sc[:, 2 * channels :] = jnp.ones((n_k, channels), BF)
    k = kv_sc[:, :channels]
    v = kv_sc[:, channels:]
    lane_head = lax.broadcasted_iota(jnp.int32, (LANES, channels), 1) // head
    scale = LOG2E / math.sqrt(head)
    zero = jnp.zeros((), BF)

    def scores(t):
        rows = q[t * LANES : (t + 1) * LANES]
        tall_q = jnp.concatenate(
            [jnp.where(lane_head == h, rows, zero) for h in range(n_heads)], axis=0
        )
        return dot_nt(tall_q, k)

    s = scores(0)
    for t in range(n_lt):
        ahead = scores(t + 1) if t + 1 < n_lt else None
        s = s * scale + bias_sc[t]
        p = jnp.exp2(s - jnp.max(s, axis=-1, keepdims=True)).astype(BF)
        o = dot(p, v)
        acc = jnp.zeros((LANES, channels), F32)
        for h in range(n_heads):
            part = o[h * LANES : (h + 1) * LANES]
            acc = jnp.where(lane_head == h, part[:, :channels] / part[:, channels:], acc)
        rows = slice(t * LANES, (t + 1) * LANES)
        gate = jax.nn.sigmoid(dot(own[rows], wg_ref[...]))
        gated = (gate * acc).astype(BF)
        res = two_ref[0, rows, :].astype(F32) + dot(gated, wo_ref[...])
        out_ref[0, rows, :] = res.astype(BF)
        s = ahead


def attention(core, own, other, two, bias, wq, wkv, wg, wo, n_heads):
    n_rows, n_q, channels = own.shape
    n_src, n_pay, _ = bias.shape
    n_lt = n_q // LANES
    row = lambda i: (i, 0, 0)
    fixed2 = lambda i: (0, 0)
    return pl.pallas_call(
        attention_kernel,
        grid=(n_rows,),
        in_specs=[
            pl.BlockSpec(memory_space=pltpu.SMEM),
            pl.BlockSpec((1, n_q, channels), row),
            pl.BlockSpec((1, n_q, channels), row),
            pl.BlockSpec((1, n_q, channels), row),
            pl.BlockSpec(bias.shape, lambda i: (0, 0, 0)),
            pl.BlockSpec(wq.shape, fixed2),
            pl.BlockSpec(wkv.shape, fixed2),
            pl.BlockSpec(wg.shape, fixed2),
            pl.BlockSpec(wo.shape, fixed2),
        ],
        out_specs=pl.BlockSpec((1, n_q, channels), row),
        out_shape=jax.ShapeDtypeStruct(own.shape, BF),
        scratch_shapes=[
            pltpu.VMEM((n_lt, n_src * n_pay, LANES), F32),
            pltpu.VMEM((n_lt, n_heads * LANES, 2 * n_q), F32),
            pltpu.VMEM((2 * n_q, 3 * channels), BF),
        ],
        name="attention",
    )(core, own, other, two, bias, wq, wkv, wg, wo)


def body(
    pair_in,
    coords,
    chain_ids,
    coord_mask,
    gain_tri,
    gain_sum,
    gain_attn,
    w_tri_in,
    w_tri_out,
    w_bins,
    same_chain,
    w_query,
    w_attn,
    w_bias,
    w_attn_out,
):
    n_rh, n_core, n_col = (lax.axis_size(a) for a in ("rh", "core", "col"))
    rh, core, col = (lax.axis_index(a) for a in ("rh", "core", "col"))
    n_dev = n_rh * n_core * n_col
    every = ("rh", "core", "col")
    row_count, col_count, ch = pair_in.shape
    n_heads = w_bias.shape[1]
    n_bins = w_bins.shape[0]
    sub = row_count // n_col
    half = col_count // n_core
    n_pa = n_core * sub
    n_q = n_col * half

    moved = exchange(
        pair_in.reshape(sub, n_col, n_core, half, ch)
        .transpose(2, 1, 0, 3, 4)
        .reshape(n_core * n_col, sub, half, ch),
        ("core", "col"),
    ).reshape(n_core, n_col, sub, half, ch)

    packed = jnp.concatenate(
        [coords, chain_ids.astype(F32)[None], coord_mask.astype(F32)[None]], axis=0
    )
    known = exchange(
        jnp.broadcast_to(packed, (n_rh * n_core, *packed.shape)), ("rh", "core")
    ).reshape(n_rh, n_core, -1, row_count)
    near = lax.dynamic_index_in_dim(known, rh, 0, keepdims=False)
    near = near.transpose(1, 0, 2).reshape(-1, n_core, sub, n_col)
    near = lax.dynamic_index_in_dim(near, col, 3, keepdims=False).reshape(-1, n_pa)
    far = lax.dynamic_index_in_dim(known, core, 1, keepdims=False)
    far = far.transpose(0, 2, 1).reshape(n_q, -1)

    sides = exchange(make_sides(pair_in, gain_tri, w_tri_in[:, : 4 * ch].T), every)
    back = exchange(triangle(sides, n_rh, n_core, n_col, row_count, col_count), every)
    two, normed, bias = update(
        back,
        moved,
        near,
        far,
        (gain_tri.reshape(1, ch), gain_sum.reshape(ch, 1), gain_attn.reshape(1, ch)),
        w_tri_in[:, 4 * ch :],
        w_tri_out,
        jnp.pad(w_bins, ((0, ch - n_bins), (0, 0))),
        same_chain.reshape(1, ch),
        jnp.pad(w_bias.T, ((0, 16 - n_heads), (0, 0))),
        n_heads,
        n_bins,
    )

    n_pay = sub * n_heads
    spread = exchange(
        jnp.broadcast_to(
            bias.reshape(1, n_core, 1, n_pay, n_q), (n_rh, n_core, n_col, n_pay, n_q)
        ).reshape(n_dev, n_pay, n_q),
        every,
    )
    other = lax.ppermute(normed, every, [(d, d ^ n_col) for d in range(n_dev)])
    result = attention(
        core.reshape(1),
        normed,
        other,
        two,
        spread,
        w_query,
        w_attn[:, : 2 * ch],
        w_attn[:, 2 * ch :],
        w_attn_out,
        n_heads,
    )
    home = exchange(
        result.reshape(n_core, sub, n_col, half, ch)
        .transpose(0, 2, 1, 3, 4)
        .reshape(n_core * n_col, sub, half, ch),
        ("core", "col"),
    )
    return (
        home.reshape(n_core, n_col, sub, half, ch)
        .transpose(2, 1, 0, 3, 4)
        .reshape(row_count, col_count, ch)
    )


def solution(mesh):
    n_row, n_col = mesh.shape["row"], mesh.shape["col"]
    split = Mesh(mesh.devices.reshape(n_row // 2, 2, n_col), ("rh", "core", "col"))
    row = ("rh", "core")
    return jax.shard_map(
        body,
        mesh=split,
        in_specs=(P(row, "col", None), P(None, row), P(row), P(row)) + (P(),) * 11,
        out_specs=P(row, "col", None),
        check_vma=False,
    )
```

time: 273 us -> 240 us (0.88)
  other arithmetic: 34.3 us -> 1.95 us
  Pallas kernels: 41 us -> 71.1 us
  local copies, waits for them, and re-layouts: 40.7 us -> 22 us
  matrix products: 12.9 us -> 0 us
  waiting for transfers between devices: 84.5 us -> 88.4 us
  starting transfers between devices: 35.2 us -> 32.4 us
    pallas_call x1 -> x4, Pallas kernels: 41 us -> 71.1 us  [the longest x1 37.6 us: attention(): pl.pallas_call(attention_kernel, grid=(n_rows,), in_specs=[pl.BlockSpec(m...]
    convert_element_type x8 -> x0, other arithmetic: 17.9 us -> none  [the longest x1 6.42 us: body(): left = (jax.nn.sigmoid(proj[:, :ch]) * proj[:, ch:2 * ch]).astype(BF)]
    dot_general x6 -> x0, matrix products: 12.9 us -> none  [the longest x3 7.64 us: dot(): return jnp.dot(a, b, preferred_element_type=F32)]
    transpose x5 -> x1, local copies, waits for them, and re-layouts: 9.93 us -> 0.83 us  [body(): far = far.transpose(0, 2, 1).reshape(n_q, -1)]
    reduce_sum x8 -> x0, other arithmetic: 8.78 us -> none  [the longest x4 5.99 us: layer_norm(): spread = jnp.mean(center * center, axis=-1, keepdims=True)]
    reshape x5 -> x2, local copies, waits for them, and re-layouts: 9.81 us -> 1.4 us  [the longest x1 0.73 us: body(): gain_sum.reshape(ch, 1)]
    unnamed x28 -> x21, local copies, waits for them, and re-layouts: 1.07 us -> 6.5 us
    all_to_all x5, waiting for transfers between devices: 83.2 us -> 88.4 us  [exchange(): return lax.all_to_all(x, axes, split_axis=0, concat_axis=0, tiled=True)]
  transfers between devices with their start and end apart: 6 -> 6, of which waited for: 5 -> 4; matrix products, arithmetic and copies ran while one was open for 15% -> 5% of each run, Pallas kernels for 0% -> 8%
where the time goes in v2:
time: 240 us; the launch traced here: 239 us
  waiting for transfers between devices  88.4 us (37%)
  Pallas kernels  71.1 us (30%)
  starting transfers between devices  32.4 us (14%)
  blocking collectives  23.2 us (10%)
  local copies, waits for them, and re-layouts  22 us (9%)
    all_to_all x5, waiting for transfers between devices, exchange(): return lax.all_to_all(x, axes, split_axis=0, concat_axis=0, tiled=True)  88.4 us
    pallas_call x1, Pallas kernels, attention(): pl.pallas_call(attention_kernel, grid=(n_rows,), in_specs=[pl.BlockSpec(m...  37.6 us
    all_to_all x5, starting transfers between devices, exchange(): return lax.all_to_all(x, axes, split_axis=0, concat_axis=0, tiled=True)  31.1 us
    all_to_all x1, blocking collectives, exchange(): return lax.all_to_all(x, axes, split_axis=0, concat_axis=0, tiled=True)  23.2 us
    pallas_call x1, Pallas kernels, update(): pl.pallas_call(functools.partial(update_kernel, n_bins), grid=(n_pa,), in...  15.3 us
    pallas_call x1, Pallas kernels, make_sides(): pl.pallas_call(sides_kernel, out_shape=jax.ShapeDtypeStruct((ch, n_out, L...  12.1 us
    unnamed x21, local copies, waits for them, and re-layouts  6.5 us
    pallas_call x1, Pallas kernels, triangle(): pl.pallas_call(functools.partial(triangle_kernel, n_rh, n_core, n_col, n_...  6.02 us
  transfers between devices with their start and end apart: 6, of which 4 were waited for; matrix products, arithmetic and copies ran while one was open for 5% of the time, Pallas kernels for 8%

profile of v2, /device:TPU:1, one launch (start us, length us, event | category | flops | bytes accessed | tf_op | source)
XLA Modules:
  0.0 239.1 jit_solution(18115986213231167194)
XLA Ops:
  0.0 0.7 convert_bitcast_fusion
  0.7 0.7 pad_maximum_fusion
  1.4 0.7 reshape.73
  2.1 6.8 %all-to-all-start.3 = ((f32[16,1,240]{2,1,0:T(1,128)}), f32[16,1,240]{2,1,0:T(1,128)S(1)}, u32[]{:S(2)}, u32[]{:S(2)}) async-start(f32[16,1,240]{2,1,0:T(1,128)} %reshape.73), calls=%async_computation.3 | async-start | bytes 32768 | tf_op jit(solution)/shard_map/all_to_all | solution.py:34
  8.9 0.9 slice.12
  9.8 0.8 copy.36
  10.6 12.1 %sides.1 = bf16[128,72,128]{2,1,0:T(8,128)(2,1)} custom-call(bf16[48,96,128]{2,1,0:T(8,128)(2,1)} %x_ref.1, f32[1,128]{1,0:T(1,128)} %bitcast.46, bf16[512,128]{1,0:T(8,128)(2,1)} %bitcast.42), custom_call_target="tpu_custom_call" | custom-call | tf_op jit(solution)/shard_map/sides/pallas_call | solution.py:99
  22.6 0.0 copy-start.4
  22.6 0.0 all-to-all-done.3
  22.6 10.2 %all-to-all-start = ((bf16[128,72,128]{2,1,0:T(8,128)(2,1)}), bf16[128,72,128]{2,1,0:T(8,128)(2,1)S(1)}, u32[]{:S(2)}, u32[]{:S(2)}) async-start(bf16[128,72,128]{2,1,0:T(8,128)(2,1)} %sides.1), calls=%async_computation | async-start | bytes 4718592 | tf_op jit(solution)/shard_map/all_to_all | solution.py:34
  32.9 0.0 copy-done.4
  32.9 1.1 copy.30
  34.0 31.5 %all-to-all-done.in_ref = bf16[128,72,128]{2,1,0:T(8,128)(2,1)S(1)} async-done(((bf16[128,72,128]{2,1,0:T(8,128)(2,1)}), bf16[128,72,128]{2,1,0:T(8,128)(2,1)S(1)}, u32[]{:S(2)}, u32[]{:S(2)}) %all-to-all-start) | async-done | bytes 2359328 | tf_op jit(solution)/shard_map/all_to_all | solution.py:34
  65.5 0.0 copy-start.1
  65.5 1.4 copy-done.1
  66.9 5.2 %all-to-all-start.2 = ((bf16[16,6,48,128]{3,2,1,0:T(8,128)(2,1)}), bf16[16,6,48,128]{3,2,1,0:T(8,128)(2,1)S(1)}, u32[]{:S(2)}, u32[]{:S(2)}) async-start(bf16[16,6,48,128]{3,2,1,0:T(8,128)(2,1)} %bitcast.37), calls=%async_computation.2 | async-start | bytes 2359296 | tf_op jit(solution)/shard_map/all_to_all | solution.py:34
  72.1 6.0 %triangle.1 = bf16[128,36,128]{2,1,0:T(8,128)(2,1)} custom-call(bf16[128,72,128]{2,1,0:T(8,128)(2,1)} %copy-done.1), custom_call_target="tpu_custom_call" | custom-call | tf_op jit(solution)/shard_map/triangle/pallas_call | solution.py:165
  78.1 0.0 copy-start.8
  78.1 0.0 copy-start.6
  78.1 0.0 copy-start.7
  78.1 13.1 %all-to-all-done.2 = bf16[16,6,48,128]{3,2,1,0:T(8,128)(2,1)S(1)} async-done(((bf16[16,6,48,128]{3,2,1,0:T(8,128)(2,1)}), bf16[16,6,48,128]{3,2,1,0:T(8,128)(2,1)S(1)}, u32[]{:S(2)}, u32[]{:S(2)}) %all-to-all-start.2) | async-done | bytes 1179680 | tf_op jit(solution)/shard_map/all_to_all | solution.py:34
  91.2 0.0 copy-start.3
  91.2 1.0 copy-done.3
  92.2 3.8 %all-to-all-start.1 = ((bf16[128,36,128]{2,1,0:T(8,128)(2,1)}), bf16[128,36,128]{2,1,0:T(8,128)(2,1)S(1)}, u32[]{:S(2)}, u32[]{:S(2)}) async-start(bf16[128,36,128]{2,1,0:T(8,128)(2,1)} %triangle.1), calls=%async_computation.1 | async-start | bytes 2621440 | tf_op jit(solution)/shard_map/all_to_all | solution.py:34
  96.0 1.4 slice.13.wgo_ref
  97.4 0.0 copy-done.8
  97.4 0.7 copy.33.gain_sum_ref
  98.1 0.0 copy-done.6
  98.1 0.6 pad.8.wbins_ref
  98.7 0.0 copy-done.7
  98.7 0.6 pad.9.wbias_ref
  99.3 0.5 broadcast.5
  99.8 0.6 reduce.2
  100.4 0.1 reshape.74
  100.5 0.1 reshape.61
  100.6 0.2 dynamic-slice_reduce_fusion
  100.8 0.7 reshape.62.near_ref
  101.5 0.8 copy.32
  102.3 15.3 %all-to-all-done.1.back_ref = bf16[128,36,128]{2,1,0:T(8,128)(2,1)S(1)} async-done(((bf16[128,36,128]{2,1,0:T(8,128)(2,1)}), bf16[128,36,128]{2,1,0:T(8,128)(2,1)S(1)}, u32[]{:S(2)}, u32[]{:S(2)}) %all-to-all-start.1) | async-done | bytes 1179680 | tf_op jit(solution)/shard_map/all_to_all | solution.py:34
  117.5 0.0 copy-start.2
  117.6 1.1 copy-done.2
  118.6 15.3 %update.1 = (bf16[12,384,128]{2,1,0:T(8,128)(2,1)}, bf16[12,384,128]{2,1,0:T(8,128)(2,1)}, bf16[12,4,384]{2,1,0:T(4,128)(2,1)}) custom-call(bf16[128,36,128]{2,1,0:T(8,128)(2,1)} %copy-done.2, bf16[2,8,6,48,128]{4,3,2,1,0:T(8,128)(2,1)} %bitcast.36, f32[5,12]{1,0:T(8,128)} %reshape.62.near_ref, f32[384,5]{1,0:T(8,128)} %bitcast.41, f32[1,128]{1,0:T(1,128)} %bitcast.47, ...), custom_call_target="tpu_custom_call" | custom-call | tf_op jit(solution)/shard_map/update/pallas_call | solution.py:255
  134.0 0.8 broadcast_in_dim.19
  134.7 1.8 broadcast_in_dim.20
  136.5 0.0 copy-start.5
  136.5 5.1 %all-to-all-start.4 = ((bf16[128,24,384]{2,1,0:T(8,128)(2,1)}), bf16[128,24,384]{2,1,0:T(8,128)(2,1)S(1)}, u32[]{:S(2)}, u32[]{:S(2)}) async-start(bf16[128,24,384]{2,1,0:T(8,128)(2,1)} %bitcast.34), calls=%async_computation.4 | async-start | bytes 4718592 | tf_op jit(solution)/shard_map/all_to_all | solution.py:34
  141.6 0.0 copy-done.5
  141.6 1.3 collective-permute-start
  142.9 1.5 slice.14.wkv_ref
  144.4 1.4 slice.15.wg_ref
  145.7 0.0 collective-permute-done.other_ref
  145.7 28.6 %all-to-all-done.4.bias_ref = bf16[128,24,384]{2,1,0:T(8,128)(2,1)S(1)} async-done(((bf16[128,24,384]{2,1,0:T(8,128)(2,1)}), bf16[128,24,384]{2,1,0:T(8,128)(2,1)S(1)}, u32[]{:S(2)}, u32[]{:S(2)}) %all-to-all-start.4) | async-done | bytes 2359328 | tf_op jit(solution)/shard_map/all_to_all | solution.py:34
  174.3 0.0 copy-start
  174.3 1.4 copy-done
  175.8 37.6 %attention.1 = bf16[12,384,128]{2,1,0:T(8,128)(2,1)} custom-call(s32[1]{0:T(128)} %bitcast.core_ref, bf16[12,384,128]{2,1,0:T(8,128)(2,1)} %get-tuple-element.8.own_ref, bf16[12,384,128]{2,1,0:T(8,128)(2,1)} %collective-permute-done.other_ref, bf16[12,384,128]{2,1,0:T(8,128)(2,1)} %get-tuple-element.9.two_ref, bf16[128,24,384]{2,1,0:T(8,128)(2,1)} %copy-done, ...), custom_call_target="tpu_custom_call" | custom-call | tf_op jit(solution)/shard_map/attention/pallas_call | solution.py:381
  213.4 1.3 copy.34
  214.8 23.2 %all_to_all.30 = bf16[16,6,48,128]{3,2,1,0:T(8,128)(2,1)S(1)} all-to-all(bf16[16,6,48,128]{3,2,1,0:T(8,128)(2,1)S(1)} %bitcast.38), channel_id=1, replica_groups=mesh['rh'=8,'core'=2,'col'=8] {'core','col'}, dimensions={0} | all-to-all | bytes 2359296 | tf_op jit(solution)/shard_map/all_to_all | solution.py:34
  238.0 1.1 copy.35
  (4 shorter events, 0.1 us)
Async XLA Ops:
  2.1 20.6 %all-to-all-start.3 = ((f32[16,1,240]{2,1,0:T(1,128)}), f32[16,1,240]{2,1,0:T(1,128)S(1)}, u32[]{:S(2)}, u32[]{:S(2)}) async-start(f32[16,1,240]{2,1,0:T(1,128)} %reshape.73), calls=%async_computation.3 | async-start | bytes 32768 | tf_op jit(solution)/shard_map/all_to_all | solution.py:34
  22.6 10.2 %copy-start.4 = (bf16[48,96,128]{2,1,0:T(8,128)(2,1)S(1)}, bf16[48,96,128]{2,1,0:T(8,128)(2,1)}, u32[]{:S(2)}) copy-start(bf16[48,96,128]{2,1,0:T(8,128)(2,1)} %x_ref.1) | copy-start | bytes 3538948
  22.6 42.8 %all-to-all-start = ((bf16[128,72,128]{2,1,0:T(8,128)(2,1)}), bf16[128,72,128]{2,1,0:T(8,128)(2,1)S(1)}, u32[]{:S(2)}, u32[]{:S(2)}) async-start(bf16[128,72,128]{2,1,0:T(8,128)(2,1)} %sides.1), calls=%async_computation | async-start | bytes 4718592 | tf_op jit(solution)/shard_map/all_to_all | solution.py:34
  65.5 1.4 copy-start.1
  66.9 24.3 %all-to-all-start.2 = ((bf16[16,6,48,128]{3,2,1,0:T(8,128)(2,1)}), bf16[16,6,48,128]{3,2,1,0:T(8,128)(2,1)S(1)}, u32[]{:S(2)}, u32[]{:S(2)}) async-start(bf16[16,6,48,128]{3,2,1,0:T(8,128)(2,1)} %bitcast.37), calls=%async_computation.2 | async-start | bytes 2359296 | tf_op jit(solution)/shard_map/all_to_all | solution.py:34
  78.1 19.3 %copy-start.8 = (f32[128]{0:T(128)S(1)}, f32[128]{0:T(128)}, u32[]{:S(2)}) copy-start(f32[128]{0:T(128)} %param.20) | copy-start | bytes 1540
  78.1 20.0 %copy-start.6 = (f32[36,128]{1,0:T(8,128)S(1)}, f32[36,128]{1,0:T(8,128)}, u32[]{:S(2)}) copy-start(f32[36,128]{1,0:T(8,128)} %param.24) | copy-start | bytes 55300
  78.1 20.6 %copy-start.7 = (bf16[128,4]{0,1:T(4,128)(2,1)S(1)}, bf16[128,4]{0,1:T(4,128)(2,1)}, u32[]{:S(2)}) copy-start(bf16[128,4]{0,1:T(4,128)(2,1)} %param.28) | copy-start | bytes 3076
  91.2 1.0 copy-start.3
  92.2 25.4 %all-to-all-start.1 = ((bf16[128,36,128]{2,1,0:T(8,128)(2,1)}), bf16[128,36,128]{2,1,0:T(8,128)(2,1)S(1)}, u32[]{:S(2)}, u32[]{:S(2)}) async-start(bf16[128,36,128]{2,1,0:T(8,128)(2,1)} %triangle.1), calls=%async_computation.1 | async-start | bytes 2621440 | tf_op jit(solution)/shard_map/all_to_all | solution.py:34
  117.5 1.1 copy-start.2
  136.5 5.1 %copy-start.5 = (bf16[12,384,128]{2,1,0:T(8,128)(2,1)S(1)}, bf16[12,384,128]{2,1,0:T(8,128)(2,1)}, u32[]{:S(2)}) copy-start(bf16[12,384,128]{2,1,0:T(8,128)(2,1)} %get-tuple-element.8.own_ref) | copy-start | bytes 3538948
  136.5 37.8 %all-to-all-start.4 = ((bf16[128,24,384]{2,1,0:T(8,128)(2,1)}), bf16[128,24,384]{2,1,0:T(8,128)(2,1)S(1)}, u32[]{:S(2)}, u32[]{:S(2)}) async-start(bf16[128,24,384]{2,1,0:T(8,128)(2,1)} %bitcast.34), calls=%async_computation.4 | async-start | bytes 4718592 | tf_op jit(solution)/shard_map/all_to_all | solution.py:34
  141.6 4.1 %collective-permute-start = (bf16[12,384,128]{2,1,0:T(8,128)(2,1)S(1)}, bf16[12,384,128]{2,1,0:T(8,128)(2,1)}, u32[]{:S(2)}, u32[]{:S(2)}) collective-permute-start(bf16[12,384,128]{2,1,0:T(8,128)(2,1)S(1)} %copy-done.5), channel_id=1, source_target_pairs={{0,8},{1,9},{2,10},{3,11},{4,12},{5,13},{6,14},{7,15},{8,0},{9,1},... | collective-permute-start | bytes 3538952 | tf_op jit(solution)/shard_map/ppermute | solution.py:478
  174.3 1.4 copy-start
